TPU v7x, 32 devices: a whole 2x2x4 slice. The times are simulated.
32 devices in a mesh: row: 4 (over x, core), col: 8 (over z, y).
Axes of the slice: x: 2, y: 2, z: 4, core: 2. Of those that a mesh axis runs over, the one named last changes fastest.
Arguments:
- rhs: float32 [4, 8, 8, 4, 128], P('row', 'col'), may hold values from -6 to 6
- diag0: float32 [4, 8, 8, 128], P('row', 'col'), may hold values from 2 to 4
- blocks0: float32 [4, 8, 8, 14, 128, 128], P('row', 'col'), may hold values from -0.1875 to 0.1875
- cols0: int32 [4, 8, 8, 14], P('row', 'col'), may hold values from 0 to 23
- sends0: int32 [4, 8, 4, 4], P('row', 'col'), may hold values from 0 to 7
- pro0: float32 [4, 8, 8, 128, 128], P('row', 'col'), may hold values from -0.5 to 0.5
- agg0: int32 [4, 8, 8], P('row', 'col'), may hold values from 0 to 1
- diag1: float32 [4, 8, 2, 128], P('row', 'col'), may hold values from 2 to 4
- blocks1: float32 [4, 8, 2, 14, 128, 128], P('row', 'col'), may hold values from -0.1875 to 0.1875
- cols1: int32 [4, 8, 2, 14], P('row', 'col'), may hold values from 0 to 9
- sends1: int32 [4, 8, 4, 2], P('row', 'col'), may hold values from 0 to 1
- pro1: float32 [4, 8, 2, 128, 128], P('row', 'col'), may hold values from -0.25 to 0.25
- agg1: int32 [4, 8, 2], P('row', 'col'), may hold values from 0 to 7
- cinv: float32 [1024, 1024], P(('row', 'col')), may hold values from -0.1875 to 0.1875
Outputs:
- solution: float32 [4, 8, 8, 4, 128], P('row', 'col')
Inputs may be any that keep to these rules, and one draw needn't show every extreme that they name: `sends0`: indices of the sender's own fine blocks. `sends1`: indices of the sender's own level-one blocks. `cols0`: indices into the extended fine vector of 24 blocks. `cols1`: indices into the extended level-one vector of 10 blocks. `agg0`: a level-one block of the same partition. `agg1`: a coarsest block, on any partition.
All inputs are finite; a program needn't handle non-finite values.
Results may differ from a plain program's by a relative error of at most 0.0001.
Values sent between devices are 32-bit elements; how exact they have to be, the bound alone decides.
A program may use at most 64 MiB of HBM per device.

v0:
```python
import jax
import jax.numpy as jnp
from jax import lax
from jax.sharding import PartitionSpec as P

NU = 2


HIGH = lax.Precision.HIGHEST
OMEGA = 0.3


def padded_2(value, sides, width):
    for axis, dim in sides:
        size, length = (lax.axis_size(axis), value.shape[dim])
        up = [(i, (i + 1) % size) for i in range(size - 1)]
        down = [(j, i) for i, j in up]
        last = lax.slice_in_dim(value, length - width, length, axis=dim)
        leading = lax.slice_in_dim(value, 0, width, axis=dim)
        before = lax.ppermute(last, axis, up)
        after = lax.ppermute(leading, axis, down)
        value = jnp.concatenate([before, value, after], axis=dim)
    return value


def gather_ghosts(vector, sends):
    packed = vector[sends]
    padded = padded_2(packed[None, None], (("row", 0), ("col", 1)), 1)
    return jnp.concatenate(
        [vector, padded[0, 1, 0], padded[2, 1, 1], padded[1, 0, 2], padded[1, 2, 3]], axis=0
    )


def apply_op(vector, diag, blocks, cols, sends):
    extended = gather_ghosts(vector, sends)
    nearby = extended[cols]
    coupled = jnp.einsum("bkij,bkrj->bri", blocks, nearby, precision=HIGH)
    return diag[:, None, :] * vector + coupled


def smooth(vector, right_side, diag, blocks, cols, sends, count):
    for sweep in range(count):
        vector = (
            vector
            + OMEGA * (right_side - apply_op(vector, diag, blocks, cols, sends)) / diag[:, None, :]
        )
    return vector


def on_device(
    rhs, diag0, blocks0, cols0, sends0, pro0, agg0, diag1, blocks1, cols1, sends1, pro1, agg1, cinv
):
    fine_rhs = rhs[0, 0]
    fine_diag = diag0[0, 0]
    fine_blocks = blocks0[0, 0]
    fine_cols = cols0[0, 0]
    fine_sends = sends0[0, 0]
    fine_pro = pro0[0, 0]
    level_diag = diag1[0, 0]
    level_blocks = blocks1[0, 0]
    level_cols = cols1[0, 0]
    level_sends = sends1[0, 0]
    level_pro = pro1[0, 0]
    level_count = level_diag.shape[0]
    block_size = level_diag.shape[1]
    loads = fine_rhs.shape[1]
    coarse_total = cinv.shape[1]
    coarse_count = coarse_total // block_size
    fine_x = OMEGA * fine_rhs / fine_diag[:, None, :]
    fine_x = smooth(fine_x, fine_rhs, fine_diag, fine_blocks, fine_cols, fine_sends, NU - 1)
    fine_res = fine_rhs - apply_op(fine_x, fine_diag, fine_blocks, fine_cols, fine_sends)
    onehot0 = (agg0[0, 0][:, None] == jnp.arange(level_count)).astype(jnp.float32)
    restricted = jnp.einsum("bij,bri->brj", fine_pro, fine_res, precision=HIGH)
    level_rhs = jnp.einsum("bc,brj->crj", onehot0, restricted, precision=HIGH)
    level_x = OMEGA * level_rhs / level_diag[:, None, :]
    level_x = smooth(level_x, level_rhs, level_diag, level_blocks, level_cols, level_sends, NU - 1)
    level_res = level_rhs - apply_op(level_x, level_diag, level_blocks, level_cols, level_sends)
    onehot1 = (agg1[0, 0][:, None] == jnp.arange(coarse_count)).astype(jnp.float32)
    contrib = jnp.einsum("bij,bri->brj", level_pro, level_res, precision=HIGH)
    term = jnp.einsum("bc,brj->rcj", onehot1, contrib, precision=HIGH).reshape(loads, coarse_total)
    coarse_rhs = lax.psum(term, ("row", "col"))
    own_rows = jnp.einsum("ij,rj->ri", cinv, coarse_rhs, precision=HIGH)
    coarse_x = lax.all_gather(own_rows, ("row", "col"), axis=1, tiled=True)
    coarse_blocks = coarse_x.reshape(loads, coarse_count, block_size)
    picked = jnp.einsum("bc,rcj->brj", onehot1, coarse_blocks, precision=HIGH)
    level_x = level_x + jnp.einsum("bij,brj->bri", level_pro, picked, precision=HIGH)
    level_x = smooth(level_x, level_rhs, level_diag, level_blocks, level_cols, level_sends, NU)
    lifted = jnp.einsum("bc,crj->brj", onehot0, level_x, precision=HIGH)
    fine_x = fine_x + jnp.einsum("bij,brj->bri", fine_pro, lifted, precision=HIGH)
    fine_x = smooth(fine_x, fine_rhs, fine_diag, fine_blocks, fine_cols, fine_sends, NU)
    return fine_x[None, None]


def solution(mesh):
    return jax.shard_map(
        on_device,
        mesh=mesh,
        in_specs=(
            P("row", "col", None, None, None),
            P("row", "col", None, None),
            P("row", "col", None, None, None, None),
            P("row", "col", None, None),
            P("row", "col", None, None),
            P("row", "col", None, None, None),
            P("row", "col", None),
            P("row", "col", None, None),
            P("row", "col", None, None, None, None),
            P("row", "col", None, None),
            P("row", "col", None, None),
            P("row", "col", None, None, None),
            P("row", "col", None),
            P(("row", "col"), None),
        ),
        out_specs=P("row", "col", None, None, None),
        check_vma=False,
    )
```

profile of v0, /device:TPU:0, one launch (start us, length us, event | category | flops | bytes accessed | tf_op | source)
XLA Modules:
  0.0 296.4 jit_solution(16686773013737030327)
XLA Ops:
  0.0 0.8 compare_select_fusion.3
  3.1 2.4 collective-permute-start
  5.5 1.3 collective-permute-start.1
  7.6 3.1 %collective-permute-done.1 = f32[1,1,4,4,4,128]{5,4,3,2,1,0:T(4,128)S(1)} collective-permute-done((f32[1,1,4,4,4,128]{5,4,3,2,1,0:T(4,128)S(1)}, f32[1,1,4,4,4,128]{5,4,3,2,1,0:T(4,128)S(1)}, u32[]{:S(2)}, u32[]{:S(2)}) %collective-permute-start.1) | collective-permute-done | bytes 32800 | tf_op jit(solution)/shard_map/ppermute | solution.py:21
  10.8 3.4 %collective-permute-start.2 = (f32[3,1,4,4,4,128]{5,4,3,2,1,0:T(4,128)S(1)}, f32[3,1,4,4,4,128]{5,4,3,2,1,0:T(4,128)S(1)}, u32[]{:S(2)}, u32[]{:S(2)}) collective-permute-start(f32[3,1,4,4,4,128]{5,4,3,2,1,0:T(4,128)S(1)} %pad_maximum_fusion), channel_id=1, source_target_pairs={{0,1},{1,2},{2,3},{3,4},{4,5},{5,6},{6,7},{8,9},{9,10},{10,11},{11... | collective-permute-start | bytes 294920 | tf_op jit(solution)/shard_map/ppermute | solution.py:20
  14.2 1.3 collective-permute-start.3
  15.5 0.9 collective-permute-done.2
  16.4 4.3 %collective-permute-done.3 = f32[3,1,4,4,4,128]{5,4,3,2,1,0:T(4,128)S(1)} collective-permute-done((f32[3,1,4,4,4,128]{5,4,3,2,1,0:T(4,128)S(1)}, f32[3,1,4,4,4,128]{5,4,3,2,1,0:T(4,128)S(1)}, u32[]{:S(2)}, u32[]{:S(2)}) %collective-permute-start.3) | collective-permute-done | bytes 98336 | tf_op jit(solution)/shard_map/ppermute | solution.py:21
  21.5 8.3 %constant_dynamic-update-slice_fusion.9 = (f32[24,4,128]{2,1,0:T(4,128)S(1)}, f32[8,4,128]{2,1,0:T(4,128)S(1)}) fusion(f32[8,14,4,128]{3,2,1,0:T(4,128)S(1)} %bitcast.438, f32[1,1,8,14,128,128]{5,4,3,2,1,0:T(8,128)} %param.16, f32[8,128]{1,0:T(8,128)} %bitcast.466, f32[1,1,8,4,128]{4,3,2,1,0:T(4,128)} %param.14), kind=kOutput, calls=%fused_computation.94 | convolution fusion | flops 88113152 | bytes 7622656 | tf_op jit(solution)/shard_map/bkij,bkrj->bri/dot_general | solution.py:37
  30.4 3.1 %collective-permute-start.4 = (f32[1,1,4,4,4,128]{5,4,3,2,1,0:T(4,128)S(1)}, f32[1,1,4,4,4,128]{5,4,3,2,1,0:T(4,128)S(1)}, u32[]{:S(2)}, u32[]{:S(2)}) collective-permute-start(f32[1,1,4,4,4,128]{5,4,3,2,1,0:T(4,128)S(1)} %bitcast.456), channel_id=1, source_target_pairs={{0,8},{8,16},{16,24},{1,9},{9,17},{17,25},{2,10},{10,18},{18,26},{... | collective-permute-start | bytes 98312 | tf_op jit(solution)/shard_map/ppermute | solution.py:20
  33.5 1.3 collective-permute-start.5
  34.9 2.6 collective-permute-done.5
  37.6 4.3 %collective-permute-start.6 = (f32[3,1,4,4,4,128]{5,4,3,2,1,0:T(4,128)S(1)}, f32[3,1,4,4,4,128]{5,4,3,2,1,0:T(4,128)S(1)}, u32[]{:S(2)}, u32[]{:S(2)}) collective-permute-start(f32[3,1,4,4,4,128]{5,4,3,2,1,0:T(4,128)S(1)} %pad_maximum_fusion.1), channel_id=1, source_target_pairs={{0,1},{1,2},{2,3},{3,4},{4,5},{5,6},{6,7},{8,9},{9,10},{10,11},{11... | collective-permute-start | bytes 294920 | tf_op jit(solution)/shard_map/ppermute | solution.py:20
  41.9 1.3 collective-permute-start.7
  43.2 0.9 collective-permute-done.6
  44.1 4.3 %collective-permute-done.7 = f32[3,1,4,4,4,128]{5,4,3,2,1,0:T(4,128)S(1)} collective-permute-done((f32[3,1,4,4,4,128]{5,4,3,2,1,0:T(4,128)S(1)}, f32[3,1,4,4,4,128]{5,4,3,2,1,0:T(4,128)S(1)}, u32[]{:S(2)}, u32[]{:S(2)}) %collective-permute-start.7) | collective-permute-done | bytes 98336 | tf_op jit(solution)/shard_map/ppermute | solution.py:21
  49.2 8.2 %fusion.64 = f32[8,4,128]{2,1,0:T(4,128)S(1)} fusion(f32[8,14,4,128]{3,2,1,0:T(4,128)S(1)} %bitcast.440, f32[1,1,8,14,128,128]{5,4,3,2,1,0:T(8,128)} %param.16, f32[1,1,8,4,128]{4,3,2,1,0:T(4,128)S(1)} %copy-done.3, f32[8,4,128]{2,1,0:T(4,128)S(1)} %get-tuple-element.10, f32[8,128]{1,0:T(8,128)S(1)} %bitcast.467), kind=kOutput, calls=%fused_computation.50 | convolution fusion | flops 88092672 | bytes 7622656 | tf_op jit(solution)/shard_map/bkij,bkrj->bri/dot_general | solution.py:37
  58.7 3.1 %collective-permute-start.8 = (f32[1,1,4,2,4,128]{5,4,3,2,1,0:T(4,128)S(1)}, f32[1,1,4,2,4,128]{5,4,3,2,1,0:T(4,128)S(1)}, u32[]{:S(2)}, u32[]{:S(2)}) collective-permute-start(f32[1,1,4,2,4,128]{5,4,3,2,1,0:T(4,128)S(1)} %copy.90), channel_id=1, source_target_pairs={{0,8},{8,16},{16,24},{1,9},{9,17},{17,25},{2,10},{10,18},{18,26},{... | collective-permute-start | bytes 49160 | tf_op jit(solution)/shard_map/ppermute | solution.py:20
  61.8 1.3 collective-permute-start.9
  63.2 2.7 collective-permute-done.9
  65.9 3.4 %collective-permute-start.10 = (f32[3,1,4,2,4,128]{5,4,3,2,1,0:T(4,128)S(1)}, f32[3,1,4,2,4,128]{5,4,3,2,1,0:T(4,128)S(1)}, u32[]{:S(2)}, u32[]{:S(2)}) collective-permute-start(f32[3,1,4,2,4,128]{5,4,3,2,1,0:T(4,128)S(1)} %constant_dynamic-update-slice_fusion.10), channel_id=1, source_target_pairs={{0,1},{1,2},{2,3},{3,4},{4,5},{5,6},{6,7},{8,9},{9,10},{10,11},{11... | collective-permute-start | bytes 147464 | tf_op jit(solution)/shard_map/ppermute | solution.py:20
  69.3 1.3 collective-permute-start.11
  71.0 4.2 %collective-permute-done.11 = f32[3,1,4,2,4,128]{5,4,3,2,1,0:T(4,128)S(1)} collective-permute-done((f32[3,1,4,2,4,128]{5,4,3,2,1,0:T(4,128)S(1)}, f32[3,1,4,2,4,128]{5,4,3,2,1,0:T(4,128)S(1)}, u32[]{:S(2)}, u32[]{:S(2)}) %collective-permute-start.11) | collective-permute-done | bytes 49184 | tf_op jit(solution)/shard_map/ppermute | solution.py:21
  75.9 1.6 constant_dynamic-update-slice_fusion.25
  78.1 3.0 collective-permute-start.12
  81.1 1.3 collective-permute-start.13
  82.4 2.7 collective-permute-done.13
  85.1 4.3 %collective-permute-start.14 = (f32[3,1,4,2,4,128]{5,4,3,2,1,0:T(4,128)S(1)}, f32[3,1,4,2,4,128]{5,4,3,2,1,0:T(4,128)S(1)}, u32[]{:S(2)}, u32[]{:S(2)}) collective-permute-start(f32[3,1,4,2,4,128]{5,4,3,2,1,0:T(4,128)S(1)} %constant_dynamic-update-slice_fusion.18), channel_id=1, source_target_pairs={{0,1},{1,2},{2,3},{3,4},{4,5},{5,6},{6,7},{8,9},{9,10},{10,11},{11... | collective-permute-start | bytes 147464 | tf_op jit(solution)/shard_map/ppermute | solution.py:20
  89.4 1.3 collective-permute-start.15
  91.2 4.2 %collective-permute-done.15 = f32[3,1,4,2,4,128]{5,4,3,2,1,0:T(4,128)S(1)} collective-permute-done((f32[3,1,4,2,4,128]{5,4,3,2,1,0:T(4,128)S(1)}, f32[3,1,4,2,4,128]{5,4,3,2,1,0:T(4,128)S(1)}, u32[]{:S(2)}, u32[]{:S(2)}) %collective-permute-start.15) | collective-permute-done | bytes 49184 | tf_op jit(solution)/shard_map/ppermute | solution.py:21
  96.0 1.6 fusion.127
  98.2 41.2 %psum.7 = f32[4,1024]{1,0:T(4,128)S(1)} all-reduce(f32[4,1024]{1,0:T(4,128)S(1)} %bitcast.470), channel_id=1, replica_groups=mesh['row'=4,'col'=8] {'row','col'}, use_global_device_ids=true, to_apply=%region_0.0 | all-reduce | flops 4096 | bytes 32768 | tf_op jit(solution)/shard_map/psum | solution.py:81
  139.6 66.1 %all-gather = f32[32,32,4]{1,2,0:T(4,128)S(1)} all-gather(f32[1,32,4]{1,2,0:T(4,128)S(1)} %convolution_bitcast_fusion.1), channel_id=1, replica_groups=mesh['row'=4,'col'=8] {'row','col'}, dimensions={0}, use_global_device_ids=true | all-gather | bytes 16896 | tf_op jit(solution)/shard_map/all_gather | solution.py:83
  206.9 1.3 collective-permute-start.16
  208.2 1.3 collective-permute-start.17
  209.6 2.5 collective-permute-done.17
  212.1 3.7 %collective-permute-start.18 = (f32[3,1,4,2,4,128]{5,4,3,2,1,0:T(4,128)S(1)}, f32[3,1,4,2,4,128]{5,4,3,2,1,0:T(4,128)S(1)}, u32[]{:S(2)}, u32[]{:S(2)}) collective-permute-start(f32[3,1,4,2,4,128]{5,4,3,2,1,0:T(4,128)S(1)} %constant_dynamic-update-slice_fusion.26), channel_id=1, source_target_pairs={{0,1},{1,2},{2,3},{3,4},{4,5},{5,6},{6,7},{8,9},{9,10},{10,11},{11... | collective-permute-start | bytes 147464 | tf_op jit(solution)/shard_map/ppermute | solution.py:20
  215.8 1.3 collective-permute-start.19
  217.5 4.2 %collective-permute-done.19 = f32[3,1,4,2,4,128]{5,4,3,2,1,0:T(4,128)S(1)} collective-permute-done((f32[3,1,4,2,4,128]{5,4,3,2,1,0:T(4,128)S(1)}, f32[3,1,4,2,4,128]{5,4,3,2,1,0:T(4,128)S(1)}, u32[]{:S(2)}, u32[]{:S(2)}) %collective-permute-start.19) | collective-permute-done | bytes 49184 | tf_op jit(solution)/shard_map/ppermute | solution.py:21
  222.3 1.6 constant_dynamic-update-slice_fusion.41
  224.6 3.0 collective-permute-start.20
  227.5 1.3 collective-permute-start.21
  228.9 2.7 collective-permute-done.21
  231.6 2.8 collective-permute-start.22
  234.4 1.3 collective-permute-start.23
  236.1 4.2 %collective-permute-done.23 = f32[3,1,4,2,4,128]{5,4,3,2,1,0:T(4,128)S(1)} collective-permute-done((f32[3,1,4,2,4,128]{5,4,3,2,1,0:T(4,128)S(1)}, f32[3,1,4,2,4,128]{5,4,3,2,1,0:T(4,128)S(1)}, u32[]{:S(2)}, u32[]{:S(2)}) %collective-permute-start.23) | collective-permute-done | bytes 49184 | tf_op jit(solution)/shard_map/ppermute | solution.py:21
  241.0 1.6 fusion.106
  242.8 0.9 constant_dynamic-update-slice_fusion.46
  244.4 3.0 collective-permute-start.24
  247.3 1.3 collective-permute-start.25
  248.6 2.7 collective-permute-done.25
  251.4 2.8 collective-permute-start.26
  254.2 1.3 collective-permute-start.27
  255.6 0.9 collective-permute-done.26
  256.4 4.3 %collective-permute-done.27 = f32[3,1,4,4,4,128]{5,4,3,2,1,0:T(4,128)S(1)} collective-permute-done((f32[3,1,4,4,4,128]{5,4,3,2,1,0:T(4,128)S(1)}, f32[3,1,4,4,4,128]{5,4,3,2,1,0:T(4,128)S(1)}, u32[]{:S(2)}, u32[]{:S(2)}) %collective-permute-start.27) | collective-permute-done | bytes 98336 | tf_op jit(solution)/shard_map/ppermute | solution.py:21
  261.5 8.2 %constant_dynamic-update-slice_fusion.51 = (f32[24,4,128]{2,1,0:T(4,128)S(1)}, f32[8,4,128]{2,1,0:T(4,128)S(1)}) fusion(f32[8,4,128]{2,1,0:T(4,128)S(1)} %get-tuple-element.18, f32[8,14,4,128]{3,2,1,0:T(4,128)S(1)} %bitcast.437, f32[1,1,8,14,128,128]{5,4,3,2,1,0:T(8,128)} %param.16, f32[8,128]{1,0:T(8,128)S(1)} %bitcast.468, ...), kind=kOutput, calls=%fused_computation.136 | convolution fusion | flops 88104960 | bytes 7639040 | tf_op jit(solution)/shard_map/bkij,bkrj->bri/dot_general | solution.py:37
  270.3 3.1 %collective-permute-start.28 = (f32[1,1,4,4,4,128]{5,4,3,2,1,0:T(4,128)S(1)}, f32[1,1,4,4,4,128]{5,4,3,2,1,0:T(4,128)S(1)}, u32[]{:S(2)}, u32[]{:S(2)}) collective-permute-start(f32[1,1,4,4,4,128]{5,4,3,2,1,0:T(4,128)S(1)} %bitcast.459), channel_id=1, source_target_pairs={{0,8},{8,16},{16,24},{1,9},{9,17},{17,25},{2,10},{10,18},{18,26},{... | collective-permute-start | bytes 98312 | tf_op jit(solution)/shard_map/ppermute | solution.py:20
  273.4 1.3 collective-permute-start.29
  274.7 2.7 collective-permute-done.29
  277.5 2.8 collective-permute-start.30
  280.3 1.3 collective-permute-start.31
  281.6 0.9 collective-permute-done.30
  282.5 4.3 %collective-permute-done.31 = f32[3,1,4,4,4,128]{5,4,3,2,1,0:T(4,128)S(1)} collective-permute-done((f32[3,1,4,4,4,128]{5,4,3,2,1,0:T(4,128)S(1)}, f32[3,1,4,4,4,128]{5,4,3,2,1,0:T(4,128)S(1)}, u32[]{:S(2)}, u32[]{:S(2)}) %collective-permute-start.31) | collective-permute-done | bytes 98336 | tf_op jit(solution)/shard_map/ppermute | solution.py:21
  287.6 8.8 %fusion.43 = f32[1,1,8,4,128]{4,3,2,1,0:T(4,128)} fusion(f32[8,4,128]{2,1,0:T(4,128)S(1)} %get-tuple-element.20, f32[8,14,4,128]{3,2,1,0:T(4,128)S(1)} %bitcast.439, f32[1,1,8,14,128,128]{5,4,3,2,1,0:T(8,128)} %param.16, f32[1,1,8,4,128]{4,3,2,1,0:T(4,128)S(1)} %copy-done.3, f32[8,128]{1,0:T(8,128)S(1)} %bitcast.469), kind=kOutput, calls=%fused_computation.43 | convolution fusion | flops 88104960 | bytes 7622656 | tf_op jit(solution)/shard_map/bkij,bkrj->bri/dot_general | solution.py:37
  (128 shorter events, 17.0 us)
Async XLA Ops:
  0.0 75.9 %copy-start = (f32[1,1,2,14,128,128]{5,4,3,2,1,0:T(8,128)S(1)}, f32[1,1,2,14,128,128]{5,4,3,2,1,0:T(8,128)}, u32[]{:S(2)}) copy-start(f32[1,1,2,14,128,128]{5,4,3,2,1,0:T(8,128)} %param.22) | copy-start | bytes 5505028
  0.0 49.2 %copy-start.3 = (f32[1,1,8,4,128]{4,3,2,1,0:T(4,128)S(1)}, f32[1,1,8,4,128]{4,3,2,1,0:T(4,128)}, u32[]{:S(2)}) copy-start(f32[1,1,8,4,128]{4,3,2,1,0:T(4,128)} %param.14) | copy-start | bytes 49156
  0.0 49.2 %copy-start.5 = (f32[1,1,8,128]{3,2,1,0:T(8,128)S(1)}, f32[1,1,8,128]{3,2,1,0:T(8,128)}, u32[]{:S(2)}) copy-start(f32[1,1,8,128]{3,2,1,0:T(8,128)} %param.15) | copy-start | bytes 12292
  0.0 34.8 %copy-start.8 = (s32[1,1,2,14]{3,2,1,0:T(2,128)S(1)}, s32[1,1,2,14]{3,2,1,0:T(2,128)}, u32[]{:S(2)}) copy-start(s32[1,1,2,14]{3,2,1,0:T(2,128)} %param.23) | copy-start | bytes 340
  3.1 4.5 %collective-permute-start = (f32[1,1,4,4,4,128]{5,4,3,2,1,0:T(4,128)S(1)}, f32[1,1,4,4,4,128]{5,4,3,2,1,0:T(4,128)S(1)}, u32[]{:S(2)}, u32[]{:S(2)}) collective-permute-start(f32[1,1,4,4,4,128]{5,4,3,2,1,0:T(4,128)S(1)} %bitcast.453), channel_id=1, source_target_pairs={{0,8},{8,16},{16,24},{1,9},{9,17},{17,25},{2,10},{10,18},{18,26},{... | collective-permute-start | bytes 98312 | tf_op jit(solution)/shard_map/ppermute | solution.py:20
  5.5 5.2 %collective-permute-start.1 = (f32[1,1,4,4,4,128]{5,4,3,2,1,0:T(4,128)S(1)}, f32[1,1,4,4,4,128]{5,4,3,2,1,0:T(4,128)S(1)}, u32[]{:S(2)}, u32[]{:S(2)}) collective-permute-start(f32[1,1,4,4,4,128]{5,4,3,2,1,0:T(4,128)S(1)} %bitcast.454), channel_id=1, source_target_pairs={{8,0},{16,8},{24,16},{9,1},{17,9},{25,17},{10,2},{18,10},{26,18},{... | collective-permute-start | bytes 98312 | tf_op jit(solution)/shard_map/ppermute | solution.py:21
  10.8 5.6 %collective-permute-start.2 = (f32[3,1,4,4,4,128]{5,4,3,2,1,0:T(4,128)S(1)}, f32[3,1,4,4,4,128]{5,4,3,2,1,0:T(4,128)S(1)}, u32[]{:S(2)}, u32[]{:S(2)}) collective-permute-start(f32[3,1,4,4,4,128]{5,4,3,2,1,0:T(4,128)S(1)} %pad_maximum_fusion), channel_id=1, source_target_pairs={{0,1},{1,2},{2,3},{3,4},{4,5},{5,6},{6,7},{8,9},{9,10},{10,11},{11... | collective-permute-start | bytes 294920 | tf_op jit(solution)/shard_map/ppermute | solution.py:20
  14.2 6.5 %collective-permute-start.3 = (f32[3,1,4,4,4,128]{5,4,3,2,1,0:T(4,128)S(1)}, f32[3,1,4,4,4,128]{5,4,3,2,1,0:T(4,128)S(1)}, u32[]{:S(2)}, u32[]{:S(2)}) collective-permute-start(f32[3,1,4,4,4,128]{5,4,3,2,1,0:T(4,128)S(1)} %pad_maximum_fusion), channel_id=1, source_target_pairs={{1,0},{2,1},{3,2},{4,3},{5,4},{6,5},{7,6},{9,8},{10,9},{11,10},{12... | collective-permute-start | bytes 294920 | tf_op jit(solution)/shard_map/ppermute | solution.py:21
  21.4 36.0 %copy-start.1 = (f32[1,1,8,128,128]{4,3,2,1,0:T(8,128)S(1)}, f32[1,1,8,128,128]{4,3,2,1,0:T(8,128)}, u32[]{:S(2)}) copy-start(f32[1,1,8,128,128]{4,3,2,1,0:T(8,128)} %param.19) | copy-start | bytes 1572868
  21.5 36.5 %copy-start.7 = (s32[1,1,8]{2,1,0:T(1,128)S(1)}, s32[1,1,8]{2,1,0:T(1,128)}, u32[]{:S(2)}) copy-start(s32[1,1,8]{2,1,0:T(1,128)} %param.20) | copy-start | bytes 100
  21.5 36.6 %copy-start.6 = (f32[1,1,2,128]{3,2,1,0:T(2,128)S(1)}, f32[1,1,2,128]{3,2,1,0:T(2,128)}, u32[]{:S(2)}) copy-start(f32[1,1,2,128]{3,2,1,0:T(2,128)} %param.21) | copy-start | bytes 3076
  29.8 67.9 %copy-start.2 = (f32[1,1,2,128,128]{4,3,2,1,0:T(8,128)S(1)}, f32[1,1,2,128,128]{4,3,2,1,0:T(8,128)}, u32[]{:S(2)}) copy-start(f32[1,1,2,128,128]{4,3,2,1,0:T(8,128)} %param.25) | copy-start | bytes 393220
  29.8 68.1 %copy-start.9 = (s32[1,1,2]{2,1,0:T(1,128)S(1)}, s32[1,1,2]{2,1,0:T(1,128)}, u32[]{:S(2)}) copy-start(s32[1,1,2]{2,1,0:T(1,128)} %param.26) | copy-start | bytes 28
  29.8 109.6 %copy-start.4 = (f32[32,1024]{1,0:T(8,128)S(1)}, f32[32,1024]{1,0:T(8,128)}, u32[]{:S(2)}) copy-start(f32[32,1024]{1,0:T(8,128)} %param.27) | copy-start | bytes 393220
  30.4 4.5 %collective-permute-start.4 = (f32[1,1,4,4,4,128]{5,4,3,2,1,0:T(4,128)S(1)}, f32[1,1,4,4,4,128]{5,4,3,2,1,0:T(4,128)S(1)}, u32[]{:S(2)}, u32[]{:S(2)}) collective-permute-start(f32[1,1,4,4,4,128]{5,4,3,2,1,0:T(4,128)S(1)} %bitcast.456), channel_id=1, source_target_pairs={{0,8},{8,16},{16,24},{1,9},{9,17},{17,25},{2,10},{10,18},{18,26},{... | collective-permute-start | bytes 98312 | tf_op jit(solution)/shard_map/ppermute | solution.py:20
  33.5 4.0 %collective-permute-start.5 = (f32[1,1,4,4,4,128]{5,4,3,2,1,0:T(4,128)S(1)}, f32[1,1,4,4,4,128]{5,4,3,2,1,0:T(4,128)S(1)}, u32[]{:S(2)}, u32[]{:S(2)}) collective-permute-start(f32[1,1,4,4,4,128]{5,4,3,2,1,0:T(4,128)S(1)} %bitcast.457), channel_id=1, source_target_pairs={{8,0},{16,8},{24,16},{9,1},{17,9},{25,17},{10,2},{18,10},{26,18},{... | collective-permute-start | bytes 98312 | tf_op jit(solution)/shard_map/ppermute | solution.py:21
  37.6 6.5 %collective-permute-start.6 = (f32[3,1,4,4,4,128]{5,4,3,2,1,0:T(4,128)S(1)}, f32[3,1,4,4,4,128]{5,4,3,2,1,0:T(4,128)S(1)}, u32[]{:S(2)}, u32[]{:S(2)}) collective-permute-start(f32[3,1,4,4,4,128]{5,4,3,2,1,0:T(4,128)S(1)} %pad_maximum_fusion.1), channel_id=1, source_target_pairs={{0,1},{1,2},{2,3},{3,4},{4,5},{5,6},{6,7},{8,9},{9,10},{10,11},{11... | collective-permute-start | bytes 294920 | tf_op jit(solution)/shard_map/ppermute | solution.py:20
  41.9 6.5 %collective-permute-start.7 = (f32[3,1,4,4,4,128]{5,4,3,2,1,0:T(4,128)S(1)}, f32[3,1,4,4,4,128]{5,4,3,2,1,0:T(4,128)S(1)}, u32[]{:S(2)}, u32[]{:S(2)}) collective-permute-start(f32[3,1,4,4,4,128]{5,4,3,2,1,0:T(4,128)S(1)} %pad_maximum_fusion.1), channel_id=1, source_target_pairs={{1,0},{2,1},{3,2},{4,3},{5,4},{6,5},{7,6},{9,8},{10,9},{11,10},{12... | collective-permute-start | bytes 294920 | tf_op jit(solution)/shard_map/ppermute | solution.py:21
  58.7 4.4 %collective-permute-start.8 = (f32[1,1,4,2,4,128]{5,4,3,2,1,0:T(4,128)S(1)}, f32[1,1,4,2,4,128]{5,4,3,2,1,0:T(4,128)S(1)}, u32[]{:S(2)}, u32[]{:S(2)}) collective-permute-start(f32[1,1,4,2,4,128]{5,4,3,2,1,0:T(4,128)S(1)} %copy.90), channel_id=1, source_target_pairs={{0,8},{8,16},{16,24},{1,9},{9,17},{17,25},{2,10},{10,18},{18,26},{... | collective-permute-start | bytes 49160 | tf_op jit(solution)/shard_map/ppermute | solution.py:20
  61.8 4.0 %collective-permute-start.9 = (f32[1,1,4,2,4,128]{5,4,3,2,1,0:T(4,128)S(1)}, f32[1,1,4,2,4,128]{5,4,3,2,1,0:T(4,128)S(1)}, u32[]{:S(2)}, u32[]{:S(2)}) collective-permute-start(f32[1,1,4,2,4,128]{5,4,3,2,1,0:T(4,128)S(1)} %copy.90), channel_id=1, source_target_pairs={{8,0},{16,8},{24,16},{9,1},{17,9},{25,17},{10,2},{18,10},{26,18},{... | collective-permute-start | bytes 49160 | tf_op jit(solution)/shard_map/ppermute | solution.py:21
  65.9 5.2 %collective-permute-start.10 = (f32[3,1,4,2,4,128]{5,4,3,2,1,0:T(4,128)S(1)}, f32[3,1,4,2,4,128]{5,4,3,2,1,0:T(4,128)S(1)}, u32[]{:S(2)}, u32[]{:S(2)}) collective-permute-start(f32[3,1,4,2,4,128]{5,4,3,2,1,0:T(4,128)S(1)} %constant_dynamic-update-slice_fusion.10), channel_id=1, source_target_pairs={{0,1},{1,2},{2,3},{3,4},{4,5},{5,6},{6,7},{8,9},{9,10},{10,11},{11... | collective-permute-start | bytes 147464 | tf_op jit(solution)/shard_map/ppermute | solution.py:20
  69.3 6.0 %collective-permute-start.11 = (f32[3,1,4,2,4,128]{5,4,3,2,1,0:T(4,128)S(1)}, f32[3,1,4,2,4,128]{5,4,3,2,1,0:T(4,128)S(1)}, u32[]{:S(2)}, u32[]{:S(2)}) collective-permute-start(f32[3,1,4,2,4,128]{5,4,3,2,1,0:T(4,128)S(1)} %constant_dynamic-update-slice_fusion.10), channel_id=1, source_target_pairs={{1,0},{2,1},{3,2},{4,3},{5,4},{6,5},{7,6},{9,8},{10,9},{11,10},{12... | collective-permute-start | bytes 147464 | tf_op jit(solution)/shard_map/ppermute | solution.py:21
  78.1 4.3 %collective-permute-start.12 = (f32[1,1,4,2,4,128]{5,4,3,2,1,0:T(4,128)S(1)}, f32[1,1,4,2,4,128]{5,4,3,2,1,0:T(4,128)S(1)}, u32[]{:S(2)}, u32[]{:S(2)}) collective-permute-start(f32[1,1,4,2,4,128]{5,4,3,2,1,0:T(4,128)S(1)} %copy.95), channel_id=1, source_target_pairs={{0,8},{8,16},{16,24},{1,9},{9,17},{17,25},{2,10},{10,18},{18,26},{... | collective-permute-start | bytes 49160 | tf_op jit(solution)/shard_map/ppermute | solution.py:20
  81.1 4.0 %collective-permute-start.13 = (f32[1,1,4,2,4,128]{5,4,3,2,1,0:T(4,128)S(1)}, f32[1,1,4,2,4,128]{5,4,3,2,1,0:T(4,128)S(1)}, u32[]{:S(2)}, u32[]{:S(2)}) collective-permute-start(f32[1,1,4,2,4,128]{5,4,3,2,1,0:T(4,128)S(1)} %copy.95), channel_id=1, source_target_pairs={{8,0},{16,8},{24,16},{9,1},{17,9},{25,17},{10,2},{18,10},{26,18},{... | collective-permute-start | bytes 49160 | tf_op jit(solution)/shard_map/ppermute | solution.py:21
  85.1 6.1 %collective-permute-start.14 = (f32[3,1,4,2,4,128]{5,4,3,2,1,0:T(4,128)S(1)}, f32[3,1,4,2,4,128]{5,4,3,2,1,0:T(4,128)S(1)}, u32[]{:S(2)}, u32[]{:S(2)}) collective-permute-start(f32[3,1,4,2,4,128]{5,4,3,2,1,0:T(4,128)S(1)} %constant_dynamic-update-slice_fusion.18), channel_id=1, source_target_pairs={{0,1},{1,2},{2,3},{3,4},{4,5},{5,6},{6,7},{8,9},{9,10},{10,11},{11... | collective-permute-start | bytes 147464 | tf_op jit(solution)/shard_map/ppermute | solution.py:20
  89.4 6.0 %collective-permute-start.15 = (f32[3,1,4,2,4,128]{5,4,3,2,1,0:T(4,128)S(1)}, f32[3,1,4,2,4,128]{5,4,3,2,1,0:T(4,128)S(1)}, u32[]{:S(2)}, u32[]{:S(2)}) collective-permute-start(f32[3,1,4,2,4,128]{5,4,3,2,1,0:T(4,128)S(1)} %constant_dynamic-update-slice_fusion.18), channel_id=1, source_target_pairs={{1,0},{2,1},{3,2},{4,3},{5,4},{6,5},{7,6},{9,8},{10,9},{11,10},{12... | collective-permute-start | bytes 147464 | tf_op jit(solution)/shard_map/ppermute | solution.py:21
  206.9 2.6 collective-permute-start.16
  208.2 3.8 %collective-permute-start.17 = (f32[1,1,4,2,4,128]{5,4,3,2,1,0:T(4,128)S(1)}, f32[1,1,4,2,4,128]{5,4,3,2,1,0:T(4,128)S(1)}, u32[]{:S(2)}, u32[]{:S(2)}) collective-permute-start(f32[1,1,4,2,4,128]{5,4,3,2,1,0:T(4,128)S(1)} %copy.103), channel_id=1, source_target_pairs={{8,0},{16,8},{24,16},{9,1},{17,9},{25,17},{10,2},{18,10},{26,18},{... | collective-permute-start | bytes 49160 | tf_op jit(solution)/shard_map/ppermute | solution.py:21
  212.1 5.4 %collective-permute-start.18 = (f32[3,1,4,2,4,128]{5,4,3,2,1,0:T(4,128)S(1)}, f32[3,1,4,2,4,128]{5,4,3,2,1,0:T(4,128)S(1)}, u32[]{:S(2)}, u32[]{:S(2)}) collective-permute-start(f32[3,1,4,2,4,128]{5,4,3,2,1,0:T(4,128)S(1)} %constant_dynamic-update-slice_fusion.26), channel_id=1, source_target_pairs={{0,1},{1,2},{2,3},{3,4},{4,5},{5,6},{6,7},{8,9},{9,10},{10,11},{11... | collective-permute-start | bytes 147464 | tf_op jit(solution)/shard_map/ppermute | solution.py:20
  215.8 6.0 %collective-permute-start.19 = (f32[3,1,4,2,4,128]{5,4,3,2,1,0:T(4,128)S(1)}, f32[3,1,4,2,4,128]{5,4,3,2,1,0:T(4,128)S(1)}, u32[]{:S(2)}, u32[]{:S(2)}) collective-permute-start(f32[3,1,4,2,4,128]{5,4,3,2,1,0:T(4,128)S(1)} %constant_dynamic-update-slice_fusion.26), channel_id=1, source_target_pairs={{1,0},{2,1},{3,2},{4,3},{5,4},{6,5},{7,6},{9,8},{10,9},{11,10},{12... | collective-permute-start | bytes 147464 | tf_op jit(solution)/shard_map/ppermute | solution.py:21
  224.6 4.3 %collective-permute-start.20 = (f32[1,1,4,2,4,128]{5,4,3,2,1,0:T(4,128)S(1)}, f32[1,1,4,2,4,128]{5,4,3,2,1,0:T(4,128)S(1)}, u32[]{:S(2)}, u32[]{:S(2)}) collective-permute-start(f32[1,1,4,2,4,128]{5,4,3,2,1,0:T(4,128)S(1)} %copy.108), channel_id=1, source_target_pairs={{0,8},{8,16},{16,24},{1,9},{9,17},{17,25},{2,10},{10,18},{18,26},{... | collective-permute-start | bytes 49160 | tf_op jit(solution)/shard_map/ppermute | solution.py:20
  227.5 4.0 %collective-permute-start.21 = (f32[1,1,4,2,4,128]{5,4,3,2,1,0:T(4,128)S(1)}, f32[1,1,4,2,4,128]{5,4,3,2,1,0:T(4,128)S(1)}, u32[]{:S(2)}, u32[]{:S(2)}) collective-permute-start(f32[1,1,4,2,4,128]{5,4,3,2,1,0:T(4,128)S(1)} %copy.108), channel_id=1, source_target_pairs={{8,0},{16,8},{24,16},{9,1},{17,9},{25,17},{10,2},{18,10},{26,18},{... | collective-permute-start | bytes 49160 | tf_op jit(solution)/shard_map/ppermute | solution.py:21
  231.6 4.5 %collective-permute-start.22 = (f32[3,1,4,2,4,128]{5,4,3,2,1,0:T(4,128)S(1)}, f32[3,1,4,2,4,128]{5,4,3,2,1,0:T(4,128)S(1)}, u32[]{:S(2)}, u32[]{:S(2)}) collective-permute-start(f32[3,1,4,2,4,128]{5,4,3,2,1,0:T(4,128)S(1)} %constant_dynamic-update-slice_fusion.34), channel_id=1, source_target_pairs={{0,1},{1,2},{2,3},{3,4},{4,5},{5,6},{6,7},{8,9},{9,10},{10,11},{11... | collective-permute-start | bytes 147464 | tf_op jit(solution)/shard_map/ppermute | solution.py:20
  234.4 6.0 %collective-permute-start.23 = (f32[3,1,4,2,4,128]{5,4,3,2,1,0:T(4,128)S(1)}, f32[3,1,4,2,4,128]{5,4,3,2,1,0:T(4,128)S(1)}, u32[]{:S(2)}, u32[]{:S(2)}) collective-permute-start(f32[3,1,4,2,4,128]{5,4,3,2,1,0:T(4,128)S(1)} %constant_dynamic-update-slice_fusion.34), channel_id=1, source_target_pairs={{1,0},{2,1},{3,2},{4,3},{5,4},{6,5},{7,6},{9,8},{10,9},{11,10},{12... | collective-permute-start | bytes 147464 | tf_op jit(solution)/shard_map/ppermute | solution.py:21
  244.4 4.3 %collective-permute-start.24 = (f32[1,1,4,4,4,128]{5,4,3,2,1,0:T(4,128)S(1)}, f32[1,1,4,4,4,128]{5,4,3,2,1,0:T(4,128)S(1)}, u32[]{:S(2)}, u32[]{:S(2)}) collective-permute-start(f32[1,1,4,4,4,128]{5,4,3,2,1,0:T(4,128)S(1)} %bitcast.462), channel_id=1, source_target_pairs={{0,8},{8,16},{16,24},{1,9},{9,17},{17,25},{2,10},{10,18},{18,26},{... | collective-permute-start | bytes 98312 | tf_op jit(solution)/shard_map/ppermute | solution.py:20
  247.3 4.1 %collective-permute-start.25 = (f32[1,1,4,4,4,128]{5,4,3,2,1,0:T(4,128)S(1)}, f32[1,1,4,4,4,128]{5,4,3,2,1,0:T(4,128)S(1)}, u32[]{:S(2)}, u32[]{:S(2)}) collective-permute-start(f32[1,1,4,4,4,128]{5,4,3,2,1,0:T(4,128)S(1)} %bitcast.463), channel_id=1, source_target_pairs={{8,0},{16,8},{24,16},{9,1},{17,9},{25,17},{10,2},{18,10},{26,18},{... | collective-permute-start | bytes 98312 | tf_op jit(solution)/shard_map/ppermute | solution.py:21
  251.4 5.0 %collective-permute-start.26 = (f32[3,1,4,4,4,128]{5,4,3,2,1,0:T(4,128)S(1)}, f32[3,1,4,4,4,128]{5,4,3,2,1,0:T(4,128)S(1)}, u32[]{:S(2)}, u32[]{:S(2)}) collective-permute-start(f32[3,1,4,4,4,128]{5,4,3,2,1,0:T(4,128)S(1)} %pad_maximum_fusion.2), channel_id=1, source_target_pairs={{0,1},{1,2},{2,3},{3,4},{4,5},{5,6},{6,7},{8,9},{9,10},{10,11},{11... | collective-permute-start | bytes 294920 | tf_op jit(solution)/shard_map/ppermute | solution.py:20
  254.2 6.5 %collective-permute-start.27 = (f32[3,1,4,4,4,128]{5,4,3,2,1,0:T(4,128)S(1)}, f32[3,1,4,4,4,128]{5,4,3,2,1,0:T(4,128)S(1)}, u32[]{:S(2)}, u32[]{:S(2)}) collective-permute-start(f32[3,1,4,4,4,128]{5,4,3,2,1,0:T(4,128)S(1)} %pad_maximum_fusion.2), channel_id=1, source_target_pairs={{1,0},{2,1},{3,2},{4,3},{5,4},{6,5},{7,6},{9,8},{10,9},{11,10},{12... | collective-permute-start | bytes 294920 | tf_op jit(solution)/shard_map/ppermute | solution.py:21
  270.3 4.4 %collective-permute-start.28 = (f32[1,1,4,4,4,128]{5,4,3,2,1,0:T(4,128)S(1)}, f32[1,1,4,4,4,128]{5,4,3,2,1,0:T(4,128)S(1)}, u32[]{:S(2)}, u32[]{:S(2)}) collective-permute-start(f32[1,1,4,4,4,128]{5,4,3,2,1,0:T(4,128)S(1)} %bitcast.459), channel_id=1, source_target_pairs={{0,8},{8,16},{16,24},{1,9},{9,17},{17,25},{2,10},{10,18},{18,26},{... | collective-permute-start | bytes 98312 | tf_op jit(solution)/shard_map/ppermute | solution.py:20
  273.4 4.0 %collective-permute-start.29 = (f32[1,1,4,4,4,128]{5,4,3,2,1,0:T(4,128)S(1)}, f32[1,1,4,4,4,128]{5,4,3,2,1,0:T(4,128)S(1)}, u32[]{:S(2)}, u32[]{:S(2)}) collective-permute-start(f32[1,1,4,4,4,128]{5,4,3,2,1,0:T(4,128)S(1)} %bitcast.460), channel_id=1, source_target_pairs={{8,0},{16,8},{24,16},{9,1},{17,9},{25,17},{10,2},{18,10},{26,18},{... | collective-permute-start | bytes 98312 | tf_op jit(solution)/shard_map/ppermute | solution.py:21
  277.5 5.0 %collective-permute-start.30 = (f32[3,1,4,4,4,128]{5,4,3,2,1,0:T(4,128)S(1)}, f32[3,1,4,4,4,128]{5,4,3,2,1,0:T(4,128)S(1)}, u32[]{:S(2)}, u32[]{:S(2)}) collective-permute-start(f32[3,1,4,4,4,128]{5,4,3,2,1,0:T(4,128)S(1)} %pad_maximum_fusion.3), channel_id=1, source_target_pairs={{0,1},{1,2},{2,3},{3,4},{4,5},{5,6},{6,7},{8,9},{9,10},{10,11},{11... | collective-permute-start | bytes 294920 | tf_op jit(solution)/shard_map/ppermute | solution.py:20
  280.3 6.5 %collective-permute-start.31 = (f32[3,1,4,4,4,128]{5,4,3,2,1,0:T(4,128)S(1)}, f32[3,1,4,4,4,128]{5,4,3,2,1,0:T(4,128)S(1)}, u32[]{:S(2)}, u32[]{:S(2)}) collective-permute-start(f32[3,1,4,4,4,128]{5,4,3,2,1,0:T(4,128)S(1)} %pad_maximum_fusion.3), channel_id=1, source_target_pairs={{1,0},{2,1},{3,2},{4,3},{5,4},{6,5},{7,6},{9,8},{10,9},{11,10},{12... | collective-permute-start | bytes 294920 | tf_op jit(solution)/shard_map/ppermute | solution.py:21
where the time goes:
time: 298 us; the launch traced here: 296 us
  blocking collectives  107 us (36%)
  starting transfers between devices  70.1 us (24%)
  waiting for transfers between devices  61.1 us (21%)
  matrix products  43 us (14%)
  local copies, waits for them, and re-layouts  11 us (4%)
  other arithmetic  3.06 us (1%)
    all_gather x1, blocking collectives, on_device(): coarse_x = lax.all_gather(own_rows, ('row', 'col'), axis=1, tiled=True)  66.1 us
    ppermute x16, waiting for transfers between devices, padded_2(): after = lax.ppermute(leading, axis, down)  56 us
    ppermute x16, starting transfers between devices, padded_2(): before = lax.ppermute(last, axis, up)  49.5 us
    psum x1, blocking collectives, on_device(): coarse_rhs = lax.psum(term, ('row', 'col'))  41.2 us
    dot_general x8, matrix products, apply_op(): coupled = jnp.einsum('bkij,bkrj->bri', blocks, nearby, precision=HIGH)  40 us
    ppermute x16, starting transfers between devices, padded_2(): after = lax.ppermute(leading, axis, down)  20.7 us
  transfers between devices with their start and end apart: 32, of which 24 were waited for; matrix products, arithmetic and copies ran while one was open for 0% of the time, Pallas kernels for 0%

commit v1 on v0

v1 whole, which is shorter than its diff:
```python
import functools

import jax
import jax.numpy as jnp
from jax import lax
from jax.experimental import pallas as pl
from jax.experimental.pallas import tpu as pltpu
from jax.sharding import PartitionSpec as P

NU = 2
OMEGA = 0.3
F32 = jnp.float32
BF16 = jnp.bfloat16
MESH = pl.DeviceIdType.MESH
NT = (((1,), (1,)), ((), ()))
NN = (((1,), (0,)), ((), ()))


def two_terms(value):
    head = value.astype(BF16)
    tail = (value - head.astype(F32)).astype(BF16)
    return head, tail


def stacked(value):
    head = value.astype(BF16).astype(F32)
    rows = 2 * value.shape[0]
    pad = -rows % 16
    parts = [head, value - head]
    if pad:
        parts.append(jnp.zeros((pad, value.shape[1]), F32))
    return jnp.concatenate(parts, axis=0).astype(BF16)


def product(lhs, head, tail, dims, rows):
    both = lax.dot_general(lhs, head, dims, preferred_element_type=F32) + lax.dot_general(
        lhs, tail, dims, preferred_element_type=F32
    )
    return both[:rows] + both[rows : 2 * rows]


def kernel(
    n_row, n_col,
    cols0, sends0, agg0, cols1, sends1, agg1,
    rhs_h, diag0_h, blocks0_h, pro0_h, diag1_h, blocks1_h, pro1_h, cinv_h,
    out,
    rhs, diag0, blocks0, pro0, diag1, blocks1, pro1, cinv,
    in_sem,
    head0, tail0, head1, tail1, phead0, ptail0, phead1, ptail1, chead, ctail,
    dfull0, wfull0, dfull1, wfull1,
    ext0, ext1, x0, x1, b1,
    send0, recv0, send1, recv1,
    aggf, recva, mine, recvc, xs, recvx,
    s_send0, s_recv0, s_send1, s_recv1, s_bsend, s_brecv,
):
    nb, loads, bs = rhs.shape
    nb1 = diag1.shape[0]
    k0 = blocks0.shape[1]
    k1 = blocks1.shape[1]
    g0 = send0.shape[2]
    g1 = send1.shape[2]
    n = n_row * n_col
    owned = cinv.shape[0]
    ncb = cinv.shape[1] // bs
    reps = bs // owned
    row = lax.axis_index("row")
    col = lax.axis_index("col")
    me = row * n_col + col

    def peer(step):
        other = lax.rem(me + step, n)
        return (other // n_col, lax.rem(other, n_col))

    loading = []

    def load(source, target):
        copy = pltpu.make_async_copy(source, target, in_sem.at[len(loading)])
        loading.append(copy)
        copy.start()
        return copy

    l_rhs = load(rhs_h, rhs)
    l_diag0 = load(diag0_h, diag0)
    l_blocks0 = [load(blocks0_h.at[b], blocks0.at[b]) for b in range(nb)]
    l_pro0 = load(pro0_h, pro0)
    l_diag1 = load(diag1_h, diag1)
    l_blocks1 = load(blocks1_h, blocks1)
    l_pro1 = load(pro1_h, pro1)
    l_cinv = load(cinv_h, cinv)

    recv0[...] = jnp.zeros_like(recv0)
    recv1[...] = jnp.zeros_like(recv1)

    barrier = pltpu.get_barrier_semaphore()

    def greet(step, carry):
        pl.semaphore_signal(barrier, inc=1, device_id=peer(step), device_id_type=MESH)
        return carry

    lax.fori_loop(1, n, greet, 0)

    directions = (
        (row < n_row - 1, (row + 1, col), row > 0),
        (row > 0, (row - 1, col), row < n_row - 1),
        (col < n_col - 1, (row, col + 1), col > 0),
        (col > 0, (row, col - 1), col < n_col - 1),
    )

    def halo_copy(send, recv, s_send, s_recv, e, d, there):
        return pltpu.make_async_remote_copy(
            src_ref=send.at[e, d], dst_ref=recv.at[e, d],
            send_sem=s_send.at[e, d], recv_sem=s_recv.at[e, d],
            device_id=there, device_id_type=MESH,
        )

    def pack(x, send, sends, e):
        for d in range(4):
            for g in range(send.shape[2]):
                send[e, d, g] = x[sends[d, g]]

    def start(send, recv, s_send, s_recv, e):
        for d, (goes, there, _) in enumerate(directions):
            @pl.when(goes)
            def _():
                halo_copy(send, recv, s_send, s_recv, e, d, there).start()

    def finish(send, recv, s_send, s_recv, e):
        for d, (_, there, comes) in enumerate(directions):
            @pl.when(comes)
            def _():
                halo_copy(send, recv, s_send, s_recv, e, d, (row, col)).wait_recv()

    def drain(send, recv, s_send, s_recv, e):
        for d, (goes, there, _) in enumerate(directions):
            @pl.when(goes)
            def _():
                halo_copy(send, recv, s_send, s_recv, e, d, there).wait_send()

    level0 = (send0, recv0, s_send0, s_recv0)
    level1 = (send1, recv1, s_send1, s_recv1)

    def own_ext(x, ext, count):
        for b in range(count):
            ext[b] = stacked(x[b])

    def ghost_ext(recv, ext, count, e):
        ghosts = recv.shape[2]
        for d in range(4):
            for g in range(ghosts):
                ext[count + d * ghosts + g] = stacked(recv[e, d, g])

    def coupled(b, cols, ext, head, tail, k):
        lhs = jnp.concatenate([ext[cols[b, i]] for i in range(k)], axis=1)
        return product(lhs, head[b], tail[b], NT, loads)

    def split_blocks(b, blocks, head, tail, k):
        def one(i, carry):
            h, t = two_terms(blocks[b, i])
            at = pl.ds(pl.multiple_of(i * bs, bs), bs)
            head[b, :, at] = h
            tail[b, :, at] = t
            return carry

        lax.fori_loop(0, k, one, 0)

    l_rhs.wait()
    l_diag0.wait()
    for b in range(nb):
        d = jnp.broadcast_to(diag0[b : b + 1, :], (loads, bs))
        w = OMEGA / d
        dfull0[b] = d
        wfull0[b] = w
        x0[b] = w * rhs[b]
    pack(x0, send0, sends0, 0)
    for b in range(nb1):
        aggf[b * loads : (b + 1) * loads, :] = jnp.full((loads, bs), agg1[b].astype(F32))
    recva[me] = aggf[...]
    pl.semaphore_wait(barrier, n - 1)
    start(*level0, 0)

    def everywhere(src, dst, which):
        def one(step, carry):
            pltpu.make_async_remote_copy(
                src_ref=src, dst_ref=dst.at[me],
                send_sem=s_bsend.at[which], recv_sem=s_brecv.at[which],
                device_id=peer(step), device_id_type=MESH,
            ).start()
            return carry

        lax.fori_loop(1, n, one, 0)

    def all_bytes(dst, sem):
        part = dst.at[pl.ds(0, n - 1)]
        pltpu.make_async_copy(part, part, sem).wait()

    everywhere(aggf, recva, 0)
    own_ext(x0, ext0, nb)
    for b in range(nb):
        l_blocks0[b].wait()
        split_blocks(b, blocks0, head0, tail0, k0)

    def sweep0(e, into):
        finish(*level0, e)
        ghost_ext(recv0, ext0, nb, e)
        for b in range(nb):
            c = coupled(b, cols0, ext0, head0, tail0, k0)
            v = x0[b]
            into[b] = v + wfull0[b] * (rhs[b] - (dfull0[b] * v + c))

    def sweep1(e, right, into):
        finish(*level1, e)
        ghost_ext(recv1, ext1, nb1, e)
        for b in range(nb1):
            c = coupled(b, cols1, ext1, head1, tail1, k1)
            v = x1[b]
            into[b] = v + wfull1[b] * (right[b] - (dfull1[b] * v + c))

    e0 = 0
    for _ in range(NU - 1):
        sweep0(e0, x0)
        e0 += 1
        pack(x0, send0, sends0, e0)
        start(*level0, e0)
        own_ext(x0, ext0, nb)

    l_pro0.wait()
    for b in range(nb):
        h, t = two_terms(pro0[b])
        phead0[b] = h
        ptail0[b] = t
    l_blocks1.wait()
    for b in range(nb1):
        split_blocks(b, blocks1, head1, tail1, k1)
    l_diag1.wait()
    for b in range(nb1):
        d = jnp.broadcast_to(diag1[b : b + 1, :], (loads, bs))
        dfull1[b] = d
        wfull1[b] = OMEGA / d

    finish(*level0, e0)
    ghost_ext(recv0, ext0, nb, e0)
    sums = [jnp.zeros((loads, bs), F32) for _ in range(nb1)]
    for b in range(nb):
        c = coupled(b, cols0, ext0, head0, tail0, k0)
        r = rhs[b] - (dfull0[b] * x0[b] + c)
        q = product(stacked(r), phead0[b], ptail0[b], NN, loads)
        for a in range(nb1):
            sums[a] = sums[a] + jnp.where(agg0[b] == a, q, 0.0)
    e0 += 1

    for b in range(nb1):
        b1[b] = sums[b]
        x1[b] = wfull1[b] * sums[b]
    pack(x1, send1, sends1, 0)
    start(*level1, 0)
    own_ext(x1, ext1, nb1)
    l_pro1.wait()
    for b in range(nb1):
        h, t = two_terms(pro1[b])
        phead1[b] = h
        ptail1[b] = t
    l_cinv.wait()
    h, t = two_terms(cinv[...])
    chead[...] = h
    ctail[...] = t
    e1 = 0
    for _ in range(NU - 1):
        sweep1(e1, b1, x1)
        e1 += 1
        pack(x1, send1, sends1, e1)
        start(*level1, e1)
        own_ext(x1, ext1, nb1)
    finish(*level1, e1)
    ghost_ext(recv1, ext1, nb1, e1)
    for b in range(nb1):
        c = coupled(b, cols1, ext1, head1, tail1, k1)
        r = b1[b] - (dfull1[b] * x1[b] + c)
        q = product(stacked(r), phead1[b], ptail1[b], NN, loads)
        mine[b * loads : (b + 1) * loads, :] = q
    e1 += 1

    everywhere(mine, recvc, 1)
    recvc[me] = mine[...]
    all_bytes(recva, s_brecv.at[0])
    all_bytes(recvc, s_brecv.at[1])
    index = lax.broadcasted_iota(jnp.int32, (ncb, nb1 * loads, bs), 0).astype(F32)

    def collect(d, total):
        return total + jnp.where(recva[d][None] == index, recvc[d][None], 0.0)

    total = lax.fori_loop(
        0, n, collect, jnp.zeros((ncb, nb1 * loads, bs), F32), unroll=4
    )
    pieces = []
    for c in range(ncb):
        piece = total[c, :loads]
        for b in range(1, nb1):
            piece = piece + total[c, b * loads : (b + 1) * loads]
        pieces.append(stacked(piece))
    own = product(jnp.concatenate(pieces, axis=1), chead[...], ctail[...], NT, loads)
    wide = jnp.concatenate([own] * reps, axis=1)
    lane = lax.broadcasted_iota(jnp.int32, (loads, bs), 1)
    low = lax.rem(me, reps) * owned
    xs[...] = jnp.where((lane >= low) & (lane < low + owned), wide, 0.0)
    everywhere(xs, recvx, 2)
    recvx[me] = xs[...]
    all_bytes(recvx, s_brecv.at[2])
    for b in range(nb1):
        first = agg1[b] * reps
        piece = recvx[first]
        for t in range(1, reps):
            piece = piece + recvx[first + t]
        x1[b] = x1[b] + product(stacked(piece), phead1[b], ptail1[b], NT, loads)

    for _ in range(NU):
        pack(x1, send1, sends1, e1)
        start(*level1, e1)
        own_ext(x1, ext1, nb1)
        sweep1(e1, b1, x1)
        e1 += 1

    for b in range(nb1):
        ext1[b] = stacked(x1[b])
    for b in range(nb):
        x0[b] = x0[b] + product(ext1[agg0[b]], phead0[b], ptail0[b], NT, loads)
    for i in range(NU):
        pack(x0, send0, sends0, e0)
        start(*level0, e0)
        own_ext(x0, ext0, nb)
        sweep0(e0, out if i == NU - 1 else x0)
        e0 += 1

    for e in range(e0):
        drain(*level0, e)
    for e in range(e1):
        drain(*level1, e)
    all_bytes(recva, s_bsend.at[0])
    all_bytes(recvc, s_bsend.at[1])
    all_bytes(recvx, s_bsend.at[2])


def on_device(
    rhs, diag0, blocks0, cols0, sends0, pro0, agg0, diag1, blocks1, cols1, sends1, pro1, agg1, cinv
):
    n_row, n_col = lax.axis_size("row"), lax.axis_size("col")
    n = n_row * n_col
    _, _, nb, loads, bs = rhs.shape
    nb1 = diag1.shape[2]
    k0, k1 = cols0.shape[3], cols1.shape[3]
    g0, g1 = sends0.shape[3], sends1.shape[3]
    rounds = 2 * NU
    tall = -(-2 * loads // 16) * 16
    floats = [a[0, 0] for a in (rhs, diag0, blocks0, pro0, diag1, blocks1, pro1)] + [cinv]
    ints = [a[0, 0] for a in (cols0, sends0, agg0, cols1, sends1, agg1)]
    vm = pltpu.VMEM
    dma = pltpu.SemaphoreType.DMA
    scratch = [vm(a.shape, F32) for a in floats]
    scratch += [dma((nb + 7,))]
    scratch += [vm((nb, bs, k0 * bs), BF16)] * 2
    scratch += [vm((nb1, bs, k1 * bs), BF16)] * 2
    scratch += [vm((nb, bs, bs), BF16)] * 2
    scratch += [vm((nb1, bs, bs), BF16)] * 2
    scratch += [vm(cinv.shape, BF16)] * 2
    scratch += [vm((nb, loads, bs), F32)] * 2
    scratch += [vm((nb1, loads, bs), F32)] * 2
    scratch += [vm((nb + 4 * g0, tall, bs), BF16), vm((nb1 + 4 * g1, tall, bs), BF16)]
    scratch += [vm((nb, loads, bs), F32), vm((nb1, loads, bs), F32), vm((nb1, loads, bs), F32)]
    scratch += [vm((rounds, 4, g0, loads, bs), F32)] * 2
    scratch += [vm((rounds, 4, g1, loads, bs), F32)] * 2
    scratch += [vm((nb1 * loads, bs), F32), vm((n, nb1 * loads, bs), F32)] * 2
    scratch += [vm((loads, bs), F32), vm((n, loads, bs), F32)]
    scratch += [dma((rounds, 4))] * 4 + [dma((3,))] * 2
    result = pl.pallas_call(
        functools.partial(kernel, n_row, n_col),
        out_shape=jax.ShapeDtypeStruct((nb, loads, bs), F32),
        in_specs=[pl.BlockSpec(memory_space=pltpu.SMEM)] * 6
        + [pl.BlockSpec(memory_space=pl.ANY)] * 8,
        out_specs=pl.BlockSpec(memory_space=pltpu.VMEM),
        scratch_shapes=scratch,
        compiler_params=pltpu.CompilerParams(
            collective_id=0, has_side_effects=True, vmem_limit_bytes=60 * 1024 * 1024
        ),
    )(*ints, *floats)
    return result[None, None]


def solution(mesh):
    return jax.shard_map(
        on_device,
        mesh=mesh,
        in_specs=(
            P("row", "col", None, None, None),
            P("row", "col", None, None),
            P("row", "col", None, None, None, None),
            P("row", "col", None, None),
            P("row", "col", None, None),
            P("row", "col", None, None, None),
            P("row", "col", None),
            P("row", "col", None, None),
            P("row", "col", None, None, None, None),
            P("row", "col", None, None),
            P("row", "col", None, None),
            P("row", "col", None, None, None),
            P("row", "col", None),
            P(("row", "col"), None),
        ),
        out_specs=P("row", "col", None, None, None),
        check_vma=False,
    )
```

time: 298 us -> 60.9 us (0.20)
  blocking collectives: 107 us -> 0 us
  starting transfers between devices: 70.1 us -> 0 us
  waiting for transfers between devices: 61.1 us -> 0 us
  Pallas kernels: 0 us -> 57.8 us
  matrix products: 43 us -> 0 us
  local copies, waits for them, and re-layouts: 11 us -> 2.66 us
  other arithmetic: 3.06 us -> 0 us
    ppermute x32 -> x0, starting transfers between devices: 70.1 us -> none  [the longest x16 49.5 us: padded_2(): before = lax.ppermute(last, axis, up)]
    all_gather x1 -> x0, blocking collectives: 66.1 us -> none  [on_device(): coarse_x = lax.all_gather(own_rows, ('row', 'col'), axis=1, tiled=True)]
    ppermute x32 -> x0, waiting for transfers between devices: 61.1 us -> none  [the longest x16 56 us: padded_2(): after = lax.ppermute(leading, axis, down)]
    pallas_call x0 -> x1, Pallas kernels: none -> 57.8 us  [on_device(): pl.pallas_call(functools.partial(kernel, n_row, n_col), out_shape=jax.Sha...]
    dot_general x17 -> x0, matrix products: 43 us -> none  [the longest x8 40 us: apply_op(): coupled = jnp.einsum('bkij,bkrj->bri', blocks, nearby, precision=HIGH)]
    psum x1 -> x0, blocking collectives: 41.2 us -> none  [on_device(): coarse_rhs = lax.psum(term, ('row', 'col'))]
    gather x20 -> x0, local copies, waits for them, and re-layouts: 10.1 us -> none  [the longest x8 5.32 us: apply_op(): nearby = extended[cols]]
  transfers between devices with their start and end apart: 32 -> 0, of which waited for: 24 -> 0; matrix products, arithmetic and copies ran while one was open for 0% -> 0% of each run, Pallas kernels for 0% -> 0%
where the time goes in v1:
time: 60.9 us; the launch traced here: 60.5 us
  Pallas kernels  57.8 us (95%)
  local copies, waits for them, and re-layouts  2.66 us (4%)
    pallas_call x1, Pallas kernels, on_device(): pl.pallas_call(functools.partial(kernel, n_row, n_col), out_shape=jax.Sha...  57.8 us
    squeeze x1, local copies, waits for them, and re-layouts, on_device(): ints = [a[0, 0] for a in (cols0, sends0, agg0, cols1, sends1, agg1)]  1.34 us
    unnamed x1, local copies, waits for them, and re-layouts  1.32 us

profile of v1, /device:TPU:0, one launch (start us, length us, event | category | flops | bytes accessed | tf_op | source)
XLA Modules:
  0.0 60.5 jit_solution(4023864047131690149)
XLA Ops:
  0.0 1.3 %copy.15.sends1 = s32[4,2]{1,0:T(4,128)} copy(s32[4,2]{0,1:T(2,128)} %bitcast.25) | data formatting | bytes 64 | tf_op jit(solution)/shard_map/squeeze | solution.py:354
  1.3 57.8 %shard_map.136 = f32[8,4,128]{2,1,0:T(4,128)} custom-call(s32[8,14]{1,0:T(8,128)} %bitcast.20, s32[4,4]{1,0:T(4,128)} %bitcast.22, s32[8]{0:T(128)} %bitcast.26, s32[2,14]{1,0:T(2,128)} %bitcast.23, s32[4,2]{1,0:T(4,128)} %copy.15.sends1, s32[2]{0:T(128)} %bitcast.27, f32[8,4,128]{2,1,0:T(4,128)} %bitcast.19, f32[8,128]{1,0:T(8,128)} %bitcast.21, ...), custom_call_target="tpu_custom_call" | custom-call | tf_op jit(solution)/shard_map/pallas_call | solution.py:373
  59.2 1.3 %copy.17 = f32[1,1,8,4,128]{4,3,2,1,0:T(4,128)} copy(f32[1,1,8,4,128]{4,3,2,1,0:T(4,128)} %bitcast.18) | data formatting | bytes 32768

commit v2 on v1

--- a/solution.py
+++ b/solution.py
@@ -41,12 +41,13 @@
 
 def kernel(
     n_row, n_col,
-    cols0, sends0, agg0, cols1, sends1, agg1,
+    cols0_h, sends0_h, agg0_h, cols1_h, sends1_h, agg1_h,
     rhs_h, diag0_h, blocks0_h, pro0_h, diag1_h, blocks1_h, pro1_h, cinv_h,
     out,
     rhs, diag0, blocks0, pro0, diag1, blocks1, pro1, cinv,
+    cols0, sends0, agg0, cols1, sends1, agg1,
     in_sem,
-    head0, tail0, head1, tail1, phead0, ptail0, phead1, ptail1, chead, ctail,
+    wide0, wide1, phead0, ptail0, phead1, ptail1, chead, ctail,
     dfull0, wfull0, dfull1, wfull1,
     ext0, ext1, x0, x1, b1,
     send0, recv0, send1, recv1,
@@ -79,6 +80,13 @@
         copy.start()
         return copy
 
+    l_ints = [
+        load(source, target)
+        for source, target in (
+            (sends0_h, sends0), (cols0_h, cols0), (agg1_h, agg1),
+            (agg0_h, agg0), (sends1_h, sends1), (cols1_h, cols1),
+        )
+    ]
     l_rhs = load(rhs_h, rhs)
     l_diag0 = load(diag0_h, diag0)
     l_blocks0 = [load(blocks0_h.at[b], blocks0.at[b]) for b in range(nb)]
@@ -113,10 +121,10 @@
             device_id=there, device_id_type=MESH,
         )
 
-    def pack(x, send, sends, e):
+    def pack(x, send, sends, e, flip=False):
         for d in range(4):
             for g in range(send.shape[2]):
-                send[e, d, g] = x[sends[d, g]]
+                send[e, d, g] = x[sends[g, d] if flip else sends[d, g]]
 
     def start(send, recv, s_send, s_recv, e):
         for d, (goes, there, _) in enumerate(directions):
@@ -149,19 +157,21 @@
             for g in range(ghosts):
                 ext[count + d * ghosts + g] = stacked(recv[e, d, g])
 
-    def coupled(b, cols, ext, head, tail, k):
+    def coupled(b, cols, ext, wide, k):
         lhs = jnp.concatenate([ext[cols[b, i]] for i in range(k)], axis=1)
-        return product(lhs, head[b], tail[b], NT, loads)
-
-    def split_blocks(b, blocks, head, tail, k):
+        both = lax.dot_general(lhs, wide[b], NN, preferred_element_type=F32)
+        both = both[:, :bs] + both[:, bs:]
+        return both[:loads] + both[loads : 2 * loads]
+
+    def split_blocks(b, blocks, wide, k):
         def one(i, carry):
-            h, t = two_terms(blocks[b, i])
+            h, t = two_terms(blocks[b, i].T)
             at = pl.ds(pl.multiple_of(i * bs, bs), bs)
-            head[b, :, at] = h
-            tail[b, :, at] = t
+            wide[b, at, :bs] = h
+            wide[b, at, bs:] = t
             return carry
 
-        lax.fori_loop(0, k, one, 0)
+        lax.fori_loop(0, k, one, 0, unroll=7)
 
     l_rhs.wait()
     l_diag0.wait()
@@ -171,23 +181,37 @@
         dfull0[b] = d
         wfull0[b] = w
         x0[b] = w * rhs[b]
+    for copy in l_ints:
+        copy.wait()
     pack(x0, send0, sends0, 0)
     for b in range(nb1):
-        aggf[b * loads : (b + 1) * loads, :] = jnp.full((loads, bs), agg1[b].astype(F32))
+        aggf[b : b + 1, :] = jnp.full((1, bs), agg1[b].astype(F32))
     recva[me] = aggf[...]
     pl.semaphore_wait(barrier, n - 1)
     start(*level0, 0)
 
     def everywhere(src, dst, which):
-        def one(step, carry):
+        def one(there, carry):
             pltpu.make_async_remote_copy(
                 src_ref=src, dst_ref=dst.at[me],
                 send_sem=s_bsend.at[which], recv_sem=s_brecv.at[which],
-                device_id=peer(step), device_id_type=MESH,
+                device_id=there, device_id_type=MESH,
             ).start()
             return carry
 
-        lax.fori_loop(1, n, one, 0)
+        half = n_col // 2
+        side = col // half
+
+        def far(i, carry):
+            across = (1 - side) * half + lax.rem(col + i // n_row, half)
+            return one((lax.rem(row + i, n_row), across), carry)
+
+        def near(i, carry):
+            beside = side * half + lax.rem(col + i // n_row, half)
+            return one((lax.rem(row + i, n_row), beside), carry)
+
+        lax.fori_loop(0, n_row * half, far, 0)
+        lax.fori_loop(1, n_row * half, near, 0)
 
     def all_bytes(dst, sem):
         part = dst.at[pl.ds(0, n - 1)]
@@ -195,15 +219,21 @@
 
     everywhere(aggf, recva, 0)
     own_ext(x0, ext0, nb)
-    for b in range(nb):
+    def arrive(b):
         l_blocks0[b].wait()
-        split_blocks(b, blocks0, head0, tail0, k0)
+        split_blocks(b, blocks0, wide0, k0)
+
+    early = nb
+    for b in range(early):
+        arrive(b)
 
     def sweep0(e, into):
         finish(*level0, e)
         ghost_ext(recv0, ext0, nb, e)
         for b in range(nb):
-            c = coupled(b, cols0, ext0, head0, tail0, k0)
+            if e == 0 and b + early < nb:
+                arrive(b + early)
+            c = coupled(b, cols0, ext0, wide0, k0)
             v = x0[b]
             into[b] = v + wfull0[b] * (rhs[b] - (dfull0[b] * v + c))
 
@@ -211,7 +241,7 @@
         finish(*level1, e)
         ghost_ext(recv1, ext1, nb1, e)
         for b in range(nb1):
-            c = coupled(b, cols1, ext1, head1, tail1, k1)
+            c = coupled(b, cols1, ext1, wide1, k1)
             v = x1[b]
             into[b] = v + wfull1[b] * (right[b] - (dfull1[b] * v + c))
 
@@ -230,7 +260,7 @@
         ptail0[b] = t
     l_blocks1.wait()
     for b in range(nb1):
-        split_blocks(b, blocks1, head1, tail1, k1)
+        split_blocks(b, blocks1, wide1, k1)
     l_diag1.wait()
     for b in range(nb1):
         d = jnp.broadcast_to(diag1[b : b + 1, :], (loads, bs))
@@ -241,7 +271,7 @@
     ghost_ext(recv0, ext0, nb, e0)
     sums = [jnp.zeros((loads, bs), F32) for _ in range(nb1)]
     for b in range(nb):
-        c = coupled(b, cols0, ext0, head0, tail0, k0)
+        c = coupled(b, cols0, ext0, wide0, k0)
         r = rhs[b] - (dfull0[b] * x0[b] + c)
         q = product(stacked(r), phead0[b], ptail0[b], NN, loads)
         for a in range(nb1):
@@ -251,7 +281,7 @@
     for b in range(nb1):
         b1[b] = sums[b]
         x1[b] = wfull1[b] * sums[b]
-    pack(x1, send1, sends1, 0)
+    pack(x1, send1, sends1, 0, True)
     start(*level1, 0)
     own_ext(x1, ext1, nb1)
     l_pro1.wait()
@@ -267,13 +297,13 @@
     for _ in range(NU - 1):
         sweep1(e1, b1, x1)
         e1 += 1
-        pack(x1, send1, sends1, e1)
+        pack(x1, send1, sends1, e1, True)
         start(*level1, e1)
         own_ext(x1, ext1, nb1)
     finish(*level1, e1)
     ghost_ext(recv1, ext1, nb1, e1)
     for b in range(nb1):
-        c = coupled(b, cols1, ext1, head1, tail1, k1)
+        c = coupled(b, cols1, ext1, wide1, k1)
         r = b1[b] - (dfull1[b] * x1[b] + c)
         q = product(stacked(r), phead1[b], ptail1[b], NN, loads)
         mine[b * loads : (b + 1) * loads, :] = q
@@ -286,7 +316,11 @@
     index = lax.broadcasted_iota(jnp.int32, (ncb, nb1 * loads, bs), 0).astype(F32)
 
     def collect(d, total):
-        return total + jnp.where(recva[d][None] == index, recvc[d][None], 0.0)
+        names = recva[d]
+        names = jnp.concatenate(
+            [jnp.broadcast_to(names[b : b + 1], (loads, bs)) for b in range(nb1)], axis=0
+        )
+        return total + jnp.where(names[None] == index, recvc[d][None], 0.0)
 
     total = lax.fori_loop(
         0, n, collect, jnp.zeros((ncb, nb1 * loads, bs), F32), unroll=4
@@ -299,21 +333,26 @@
         pieces.append(stacked(piece))
     own = product(jnp.concatenate(pieces, axis=1), chead[...], ctail[...], NT, loads)
     wide = jnp.concatenate([own] * reps, axis=1)
-    lane = lax.broadcasted_iota(jnp.int32, (loads, bs), 1)
-    low = lax.rem(me, reps) * owned
-    xs[...] = jnp.where((lane >= low) & (lane < low + owned), wide, 0.0)
+    group = lax.broadcasted_iota(jnp.int32, (loads, bs), 1) // owned
+    diagonal = group == lax.broadcasted_iota(jnp.int32, (loads, bs), 0)
+    xs[...] = jnp.sum(jnp.where(diagonal, wide, 0.0), axis=0, keepdims=True)
     everywhere(xs, recvx, 2)
     recvx[me] = xs[...]
     all_bytes(recvx, s_brecv.at[2])
     for b in range(nb1):
         first = agg1[b] * reps
-        piece = recvx[first]
+        parts = jnp.concatenate([recvx[first + t] for t in range(reps)], axis=0)
+        piece = jnp.where(diagonal, parts, 0.0)
         for t in range(1, reps):
-            piece = piece + recvx[first + t]
+            turned = jnp.concatenate(
+                [parts[:, bs - t * owned :], parts[:, : bs - t * owned]], axis=1
+            )
+            turned = jnp.where(diagonal, turned, 0.0)
+            piece = piece + jnp.concatenate([turned[t:], turned[:t]], axis=0)
         x1[b] = x1[b] + product(stacked(piece), phead1[b], ptail1[b], NT, loads)
 
     for _ in range(NU):
-        pack(x1, send1, sends1, e1)
+        pack(x1, send1, sends1, e1, True)
         start(*level1, e1)
         own_ext(x1, ext1, nb1)
         sweep1(e1, b1, x1)
@@ -351,13 +390,14 @@
     rounds = 2 * NU
     tall = -(-2 * loads // 16) * 16
     floats = [a[0, 0] for a in (rhs, diag0, blocks0, pro0, diag1, blocks1, pro1)] + [cinv]
-    ints = [a[0, 0] for a in (cols0, sends0, agg0, cols1, sends1, agg1)]
+    ints = [a[0, 0] for a in (cols0, sends0, agg0, cols1)]
+    ints += [sends1[0, 0].T, agg1[0, 0]]
     vm = pltpu.VMEM
     dma = pltpu.SemaphoreType.DMA
     scratch = [vm(a.shape, F32) for a in floats]
-    scratch += [dma((nb + 7,))]
-    scratch += [vm((nb, bs, k0 * bs), BF16)] * 2
-    scratch += [vm((nb1, bs, k1 * bs), BF16)] * 2
+    scratch += [pltpu.SMEM(a.shape, jnp.int32) for a in ints]
+    scratch += [dma((nb + 7 + len(ints),))]
+    scratch += [vm((nb, k0 * bs, 2 * bs), BF16), vm((nb1, k1 * bs, 2 * bs), BF16)]
     scratch += [vm((nb, bs, bs), BF16)] * 2
     scratch += [vm((nb1, bs, bs), BF16)] * 2
     scratch += [vm(cinv.shape, BF16)] * 2
@@ -367,14 +407,14 @@
     scratch += [vm((nb, loads, bs), F32), vm((nb1, loads, bs), F32), vm((nb1, loads, bs), F32)]
     scratch += [vm((rounds, 4, g0, loads, bs), F32)] * 2
     scratch += [vm((rounds, 4, g1, loads, bs), F32)] * 2
-    scratch += [vm((nb1 * loads, bs), F32), vm((n, nb1 * loads, bs), F32)] * 2
-    scratch += [vm((loads, bs), F32), vm((n, loads, bs), F32)]
+    scratch += [vm((nb1, bs), F32), vm((n, nb1, bs), F32)]
+    scratch += [vm((nb1 * loads, bs), F32), vm((n, nb1 * loads, bs), F32)]
+    scratch += [vm((1, bs), F32), vm((n, 1, bs), F32)]
     scratch += [dma((rounds, 4))] * 4 + [dma((3,))] * 2
     result = pl.pallas_call(
         functools.partial(kernel, n_row, n_col),
         out_shape=jax.ShapeDtypeStruct((nb, loads, bs), F32),
-        in_specs=[pl.BlockSpec(memory_space=pltpu.SMEM)] * 6
-        + [pl.BlockSpec(memory_space=pl.ANY)] * 8,
+        in_specs=[pl.BlockSpec(memory_space=pl.ANY)] * 14,
         out_specs=pl.BlockSpec(memory_space=pltpu.VMEM),
         scratch_shapes=scratch,
         compiler_params=pltpu.CompilerParams(

time: 60.9 us -> 53 us (0.87)
  Pallas kernels: 57.8 us -> 51.4 us
  local copies, waits for them, and re-layouts: 2.66 us -> 1.32 us
    pallas_call x1, Pallas kernels: 57.8 us -> 51.4 us  [on_device(): pl.pallas_call(functools.partial(kernel, n_row, n_col), out_shape=jax.Sha...]
    squeeze x1 -> x0, local copies, waits for them, and re-layouts: 1.34 us -> none  [on_device(): ints = [a[0, 0] for a in (cols0, sends0, agg0, cols1, sends1, agg1)]]
where the time goes in v2:
time: 53 us; the launch traced here: 52.7 us
  Pallas kernels  51.4 us (97%)
  local copies, waits for them, and re-layouts  1.32 us (2%)
    pallas_call x1, Pallas kernels, on_device(): pl.pallas_call(functools.partial(kernel, n_row, n_col), out_shape=jax.Sha...  51.4 us
    unnamed x1, local copies, waits for them, and re-layouts  1.32 us

profile of v2, /device:TPU:0, one launch (start us, length us, event | category | flops | bytes accessed | tf_op | source)
XLA Modules:
  0.0 52.7 jit_solution(11765957419498978433)
XLA Ops:
  0.0 51.4 %shard_map.136 = f32[8,4,128]{2,1,0:T(4,128)} custom-call(s32[8,14]{1,0:T(8,128)} %bitcast.22, s32[4,4]{1,0:T(4,128)} %bitcast.24, s32[8]{0:T(128)} %bitcast.28, s32[2,14]{1,0:T(2,128)} %bitcast.25, s32[2,4]{1,0:T(2,128)} %bitcast.26, s32[2]{0:T(128)} %bitcast.29, f32[8,4,128]{2,1,0:T(4,128)} %bitcast.21, f32[8,128]{1,0:T(8,128)} %bitcast.23, ...), custom_call_target="tpu_custom_call" | custom-call | tf_op jit(solution)/shard_map/pallas_call | solution.py:414
  51.4 1.3 %copy.16 = f32[1,1,8,4,128]{4,3,2,1,0:T(4,128)} copy(f32[1,1,8,4,128]{4,3,2,1,0:T(4,128)} %bitcast.20) | data formatting | bytes 32768
